TPU v7x, 32 devices: a whole 2x2x4 slice. The times are simulated.
32 devices in a mesh: seq: 8 (over z, x), mp: 4 (over y, core).
Axes of the slice: x: 2, y: 2, z: 4, core: 2. Of those that a mesh axis runs over, the one named last changes fastest.
Arguments:
- layer_in: bfloat16 [6144, 2560], P('seq'), may hold values from -6 to 6
- ssm_input: bfloat16 [6144, 5120], P('seq', 'mp'), may hold values from -6 to 6
- b_matrix: bfloat16 [6144, 128], P('seq'), may hold values from -1.796875 to 1.796875
- c_matrix: bfloat16 [6144, 128], P('seq'), may hold values from -1.796875 to 1.796875
- dt_raw: float32 [6144, 80], P('seq', 'mp'), may hold values from -2.8 to 2.8
- dt_bias: float32 [80], P('mp'), may hold values from -7 to 0
- a_log: float32 [80], P('mp'), may hold values from -8 to 3
- d_skip: float32 [80], P('mp'), may hold values from 0.5 to 1.5
- grad_out: bfloat16 [6144, 5120], P('seq', 'mp'), may hold values from -1 to 1
Outputs:
- grad_wx: float32 [2560, 5120], P('seq', 'mp')
- grad_wbc: float32 [2560, 256], P('seq', 'mp')
- grad_alog: float32 [80], P('mp')
- grad_dtbias: float32 [80], P('mp')
- grad_dskip: float32 [80], P('mp')
All inputs are finite; a program needn't handle non-finite values.
Results may differ from a plain program's by a relative error of at most 0.0063.
Values sent between devices are 32-bit elements; how exact they have to be, the bound alone decides.
A program may use at most 192 MiB of HBM per device.

v0:
```python
from functools import partial

import jax
import jax.numpy as jnp
from jax import lax
from jax.sharding import PartitionSpec as P

GROUP = 256


def entering(array, axis, combine, identity, reverse):
    devices, mine = (lax.axis_size(axis), lax.axis_index(axis))
    everything = jax.tree.map(lambda part: lax.all_gather(part, axis), array)
    start = jax.tree.map(
        lambda part, zero: jnp.broadcast_to(jnp.asarray(zero, part.dtype), part.shape),
        array,
        identity,
    )

    def lap(k, before):
        at = devices - 1 - k if reverse else k
        reached = at > mine if reverse else at < mine
        new = combine(before, jax.tree.map(lambda part: part[at], everything))
        return jax.tree.map(lambda a, b: jnp.where(reached, a, b), new, before)

    return lax.fori_loop(0, devices, lap, start)


def contract(form, left, right):
    return jnp.einsum(form, left, right, preferred_element_type=jnp.float32)


def matmul(left, right):
    return jnp.dot(left, right, preferred_element_type=jnp.float32)


def inner_first(left, right):
    return lax.dot_general(
        left, right, (((0,), (0,)), ((), ())), preferred_element_type=jnp.float32
    )


def inner_last(left, right):
    return lax.dot_general(
        left, right, (((1,), (1,)), ((), ())), preferred_element_type=jnp.float32
    )


def reverse_sum(values):
    return jnp.flip(jnp.cumsum(jnp.flip(values, 0), axis=0), 0)


def exclusive_sum(values):
    return jnp.cumsum(values, axis=0) - values


def head_rates(dt_raw, dt_bias, a_log):
    shifted = dt_raw + dt_bias[None, :]
    dt_step = jax.nn.softplus(shifted)
    gate_slope = jax.nn.sigmoid(shifted)
    decay_rate = -jnp.exp(a_log)
    return (dt_step, gate_slope, decay_rate, dt_step * decay_rate[None, :])


def block_states(ssm_input, grad_out, b_matrix, c_matrix, dt_step, log_step):
    tok_count, head_count = dt_step.shape
    head_dim = ssm_input.shape[1] // head_count
    state_width = b_matrix.shape[1]
    groups = tok_count // GROUP
    within = jnp.cumsum(log_step.reshape(groups, GROUP, head_count), axis=1)
    totals = within[:, -1, :]
    group_steps = dt_step.reshape(groups, GROUP, head_count)
    x_four = ssm_input.reshape(groups, GROUP, head_count, head_dim)
    dy_four = grad_out.reshape(groups, GROUP, head_count, head_dim)
    x_scaled = (x_four * (group_steps * jnp.exp(totals[:, None, :] - within))[..., None]).astype(
        jnp.bfloat16
    )
    y_scaled = (dy_four * jnp.exp(within)[..., None]).astype(jnp.bfloat16)
    b_three = b_matrix.reshape(groups, GROUP, state_width)
    c_three = c_matrix.reshape(groups, GROUP, state_width)
    state_parts = contract("kqhp,kqn->khpn", x_scaled, b_three)
    grad_parts = contract("kqhp,kqn->khpn", y_scaled, c_three)
    carry_state = jnp.zeros((head_count, head_dim, state_width), jnp.float32)
    starts = []
    for group_id in range(groups):
        starts.append(carry_state)
        carry_state = jnp.exp(totals[group_id])[:, None, None] * carry_state + state_parts[group_id]
    carry_grad = jnp.zeros((head_count, head_dim, state_width), jnp.float32)
    end_grads = [carry_grad] * groups
    for group_id in range(groups - 1, -1, -1):
        end_grads[group_id] = carry_grad
        carry_grad = grad_parts[group_id] + jnp.exp(totals[group_id])[:, None, None] * carry_grad
    cumulative = jnp.cumsum(log_step, axis=0)
    block_decay = jnp.exp(cumulative[-1])
    packed = (
        within,
        totals,
        x_scaled,
        y_scaled,
        jnp.stack(starts),
        jnp.stack(end_grads),
        cumulative,
    )
    return (block_decay, carry_state, carry_grad, packed)


def one_group(d_skip, group_item):
    x_c, dy_c, b_c, c_c, dt_c, within_c, total_c, start_c, end_c, xw_c, yw_c = group_item
    size_q = x_c.shape[0]
    state_width = b_c.shape[1]
    cross_bc = inner_last(c_c, b_c)
    positions = jnp.arange(size_q)
    lower_mask = positions[:, None] >= positions[None, :]
    strict = positions[:, None] > positions[None, :]
    lagged = within_c.T[:, :, None] - within_c.T[:, None, :]
    decayed = jnp.where(lower_mask[None], jnp.exp(jnp.where(lower_mask[None], lagged, 0.0)), 0.0)
    mix_matrix = (cross_bc[None] * decayed).astype(jnp.bfloat16)
    gb_intra = contract("hrs,rhp->shp", mix_matrix, dy_c)
    paired = contract("rhp,shp->hrs", dy_c, x_c) * decayed
    paired_dt = paired * dt_c.T[:, None, :]
    mixed_sum = jnp.sum(paired_dt, axis=0).astype(jnp.bfloat16)
    box_terms = jnp.where(strict[None], cross_bc[None] * paired_dt, 0.0)
    box_flow = jnp.sum(box_terms, axis=1) - jnp.sum(box_terms, axis=2)
    da_intra = (jnp.cumsum(box_flow, axis=1) - box_flow).T
    start_low = start_c.astype(jnp.bfloat16)
    end_low = end_c.astype(jnp.bfloat16)
    y_start = contract("hpn,qn->qhp", start_low, c_c) * jnp.exp(within_c)[:, :, None]
    gb_end = (
        contract("hpn,qn->qhp", end_low, b_c) * jnp.exp(total_c[None, :] - within_c)[:, :, None]
    )
    gb_local = gb_intra + gb_end
    dx_local = (dt_c[:, :, None] * gb_local + d_skip[None, :, None] * dy_c).astype(jnp.bfloat16)
    x_wide = x_c.astype(jnp.float32)
    dy_wide = dy_c.astype(jnp.float32)
    x_gb = jnp.sum(x_wide * gb_local, axis=2)
    backward_part = jnp.sum(dy_wide * y_start, axis=2)
    forward_part = dt_c * jnp.sum(x_wide * gb_end, axis=2)
    meeting = jnp.exp(total_c) * jnp.sum(end_c * start_c, axis=(1, 2))
    da_local = (
        da_intra + reverse_sum(backward_part) + exclusive_sum(forward_part) + meeting[None, :]
    )
    dc_part = matmul(mixed_sum, b_c) + matmul(
        yw_c.reshape(size_q, -1), start_low.reshape(-1, state_width)
    )
    db_part = inner_first(mixed_sum, c_c) + matmul(
        xw_c.reshape(size_q, -1), end_low.reshape(-1, state_width)
    )
    return (dx_local, jnp.concatenate([db_part, dc_part], axis=1), x_gb, da_local)


def group_local(ssm_input, grad_out, b_matrix, c_matrix, dt_step, d_skip, packed):
    within, totals, x_scaled, y_scaled, starts, end_grads, cumulative = packed
    tok_count, head_count = dt_step.shape
    groups = within.shape[0]
    head_dim = ssm_input.shape[1] // head_count
    group_items = (
        ssm_input.reshape(groups, GROUP, head_count, head_dim),
        grad_out.reshape(groups, GROUP, head_count, head_dim),
        b_matrix.reshape(groups, GROUP, -1),
        c_matrix.reshape(groups, GROUP, -1),
        dt_step.reshape(groups, GROUP, head_count),
        within,
        totals,
        starts,
        end_grads,
        x_scaled,
        y_scaled,
    )
    dx_local, dbc_local, x_gb, da_local = lax.map(partial(one_group, d_skip), group_items)
    return (
        dx_local.reshape(tok_count, -1),
        dbc_local.reshape(tok_count, -1),
        x_gb.reshape(tok_count, head_count),
        da_local.reshape(tok_count, head_count),
    )


def device_terms(ssm_input, grad_out, b_matrix, c_matrix, dt_step, cumulative, state_in, grad_in):
    tok_count, head_count = dt_step.shape
    head_dim = ssm_input.shape[1] // head_count
    state_width = b_matrix.shape[1]
    block_end = cumulative[-1]
    state_low = state_in.astype(jnp.bfloat16)
    grad_low = grad_in.astype(jnp.bfloat16)
    rise_factor = jnp.exp(cumulative)
    fall_factor = jnp.exp(block_end[None, :] - cumulative)
    x_three = ssm_input.reshape(tok_count, head_count, head_dim)
    dy_three = grad_out.reshape(tok_count, head_count, head_dim)
    y_dev = contract("hpn,tn->thp", state_low, c_matrix) * rise_factor[:, :, None]
    gb_dev = contract("hpn,tn->thp", grad_low, b_matrix) * fall_factor[:, :, None]
    dx_carry = (dt_step[:, :, None] * gb_dev).astype(jnp.bfloat16).reshape(tok_count, -1)
    x_gb = jnp.sum(x_three.astype(jnp.float32) * gb_dev, axis=2)
    backward_part = jnp.sum(dy_three.astype(jnp.float32) * y_dev, axis=2)
    forward_part = dt_step * x_gb
    meeting = jnp.exp(block_end) * jnp.sum(grad_in * state_in, axis=(1, 2))
    da_dev = reverse_sum(backward_part) + exclusive_sum(forward_part) + meeting[None, :]
    y_rise = (dy_three * rise_factor[:, :, None]).astype(jnp.bfloat16).reshape(tok_count, -1)
    x_fall = (
        (x_three * (dt_step * fall_factor)[:, :, None]).astype(jnp.bfloat16).reshape(tok_count, -1)
    )
    dc_dev = matmul(y_rise, state_low.reshape(-1, state_width))
    db_dev = matmul(x_fall, grad_low.reshape(-1, state_width))
    return (dx_carry, jnp.concatenate([db_dev, dc_dev], axis=1), x_gb, da_dev)


def head_totals(ssm_input, grad_out, dt_step, gate_slope, decay_rate, x_gb, da_all):
    tok_count, head_count = dt_step.shape
    derivative = x_gb + decay_rate[None, :] * da_all
    skip_terms = jnp.sum(
        (ssm_input.astype(jnp.float32) * grad_out.astype(jnp.float32)).reshape(
            tok_count, head_count, -1
        ),
        axis=2,
    )
    return (
        jnp.sum(dt_step * da_all, axis=0),
        jnp.sum(gate_slope * derivative, axis=0),
        jnp.sum(skip_terms, axis=0),
    )


def join_carry(earlier, later):
    return (earlier[0] * later[0], later[0][:, None, None] * earlier[1] + later[1])


def carries(block_decay, block_state, block_grad):
    identity = (jnp.ones_like(block_decay), jnp.zeros_like(block_state))
    state_in = entering((block_decay, block_state), "seq", join_carry, identity, False)[1]
    grad_in = entering((block_decay, block_grad), "seq", join_carry, identity, True)[1]
    return (state_in, grad_in)


def projection_term(layer_in, grads):
    running = inner_first(layer_in, grads[0])
    for extra_grad in grads[1:]:
        running = running + inner_first(layer_in, extra_grad)
    return running


def on_device(layer_in, ssm_input, b_matrix, c_matrix, dt_raw, dt_bias, a_log, d_skip, grad_out):
    dt_step, gate_slope, decay_rate, log_step = head_rates(dt_raw, dt_bias, a_log)
    block_decay, block_state, block_grad, packed = block_states(
        ssm_input, grad_out, b_matrix, c_matrix, dt_step, log_step
    )
    state_in, grad_in = carries(block_decay, block_state, block_grad)
    local_part = group_local(ssm_input, grad_out, b_matrix, c_matrix, dt_step, d_skip, packed)
    carried = device_terms(
        ssm_input, grad_out, b_matrix, c_matrix, dt_step, packed[6], state_in, grad_in
    )
    grad_wx = lax.psum_scatter(
        projection_term(layer_in, (local_part[0], carried[0])),
        "seq",
        scatter_dimension=0,
        tiled=True,
    )
    dbc_all = local_part[1] + carried[1]
    owned_cols = lax.psum_scatter(dbc_all, "mp", scatter_dimension=1, tiled=True).astype(
        jnp.bfloat16
    )
    grad_wbc = lax.psum_scatter(
        projection_term(layer_in, (owned_cols,)), "seq", scatter_dimension=0, tiled=True
    )
    stat_terms = head_totals(
        ssm_input,
        grad_out,
        dt_step,
        gate_slope,
        decay_rate,
        local_part[2] + carried[2],
        local_part[3] + carried[3],
    )
    rate_sum, bias_sum, skip_sum = lax.psum((stat_terms[0], stat_terms[1], stat_terms[2]), "seq")
    return (grad_wx, grad_wbc, decay_rate * rate_sum, bias_sum, skip_sum)


def solution(mesh):
    in_specs = (
        P("seq", None),
        P("seq", "mp"),
        P("seq", None),
        P("seq", None),
        P("seq", "mp"),
        P("mp"),
        P("mp"),
        P("mp"),
        P("seq", "mp"),
    )
    out_specs = (P("seq", "mp"), P("seq", "mp"), P("mp"), P("mp"), P("mp"))
    return jax.shard_map(
        on_device, mesh=mesh, in_specs=in_specs, out_specs=out_specs, check_vma=False
    )
```

profile of v0, /device:TPU:0, one launch (start us, length us, event | category | flops | bytes accessed | tf_op | source)
XLA Modules:
  0.0 549.3 jit_solution(5819640289425789130)
XLA Ops:
  12.1 4.0 copy.150
  16.1 5.2 reshape.252
  21.3 4.0 copy.143
  25.3 6.4 %reshape.246 = bf16[3,256,20,64]{1,0,3,2:T(4,128)(2,1)} reshape(bf16[768,1280]{0,1:T(8,128)(2,1)} %copy.143) | data formatting | bytes 3932160 | tf_op jit(solution)/shard_map/reshape | solution.py:158
  31.8 4.5 multiply_convert_fusion.6
  39.7 2.2 slice_add_fusion
  47.2 3.4 pad_maximum_fusion.1
  50.6 75.8 %while.46 = (s32[]{:T(128)}, bf16[3,256,20,64]{1,3,2,0:T(8,128)(2,1)}, f32[3,256,256]{2,1,0:T(8,128)}, f32[3,256,20]{1,0,2:T(4,128)}, f32[3,256,20]{1,0,2:T(4,12...) while((s32[]{:T(128)}, ...), condition=%wide.region_16.17_spmd, body=%wide.region_2.16_spmd.sunk | while | flops 748835008 | bytes 30045056 | solution.py:169
  58.5 5.0 fusion.153
  67.4 2.5 fusion.152
  83.8 5.0 fusion.153
  92.8 2.5 fusion.152
  109.0 5.0 fusion.153
  117.9 2.5 fusion.152
  126.4 4.4 copy.163
  130.8 2.8 copy.164
  138.2 22.9 %all-gather = f32[8,1,20]{2,1,0:T(1,128)S(1)} all-gather(f32[1,1,20]{2,1,0:T(1,128)S(1)} %bitcast.402), channel_id=1, replica_groups=mesh['seq'=8,'mp'=4] {'seq'}, dimensions={0}, use_global_device_ids=true | all-gather | bytes 720 | tf_op jit(solution)/shard_map/all_gather | solution.py:13
  161.1 10.4 %while.48 = (s32[]{:T(128)}, f32[20,64,128]{2,1,0:T(8,128)S(1)}, s32[]{:T(128)}, f32[8,20]{1,0:T(8,128)S(1)}, f32[8,20,64,128]{3,2,1,0:T(8,128)}, /*index=5*/s32[]{:T(128)}, s32[]{:T(128)}) while((s32[]{:T(128)}, f32[20,64,128]{2,1,0:T(8,128)S(1)}, s32[]{:T(128)}, f32[8,20]{1,0:T(8,128)S(1)}, f32[8,20,64,128]{3,2,1,0:T(8,128)}, ...), condition=%wide.region_23.24_spmd.clone, body=%wide.region_22.23_spmd.clone.sunk | while | flops 655364 | bytes 1966433 | solution.py:26
  171.5 45.6 %all-gather.4.cloned.1.call-done = f32[8,20,64,128]{3,2,1,0:T(8,128)} async-done(((f32[1,20,64,128]{3,2,1,0:T(8,128)}), f32[8,20,64,128]{3,2,1,0:T(8,128)}) %all-gather.4.cloned.1.call-update) | async-done | bytes 5242896 | tf_op jit(solution)/shard_map/all_gather | solution.py:13
  217.1 10.2 %while.47 = (s32[]{:T(128)}, f32[20,64,128]{2,1,0:T(8,128)S(1)}, s32[]{:T(128)}, f32[8,20]{1,0:T(8,128)S(1)}, f32[8,20,64,128]{3,2,1,0:T(8,128)}, /*index=5*/s32[]{:T(128)}, s32[]{:T(128)}, s32[]{:T(128)}, s32[]{:T(128)}) while((s32[]{:T(128)}, f32[20,64,128]{2,1,0:T(8,128)S(1)}, s32[]{:T(128)}, f32[8,20]{1,0:T(8,128)S(1)}, ...), condition=%wide.region_20.21_spmd.clone, body=%wide.region_19.20_spmd.clone.sunk | while | flops 655368 | bytes 1966495 | solution.py:26
  228.6 2.7 fusion.78
  233.7 3.3 copy.159
  239.2 8.4 %fusion.98 = f32[1280,2560]{1,0:T(8,128)} fusion(bf16[768,1280]{0,1:T(8,128)(2,1)S(1)} %bitcast.367, bf16[768,2560]{1,0:T(8,128)(2,1)S(1)} %copy-done.10), kind=kOutput, calls=%fused_computation.182 | convolution fusion | flops 5033164800 | bytes 19005440 | tf_op jit(solution)/shard_map/dot_general | solution.py:38
  249.2 5.8 %reduce-scatter.8.cloned.1.call-done = f32[768,64]{0,1:T(8,128)} async-done(((f32[768,256]{0,1:T(8,128)}), f32[768,64]{0,1:T(8,128)}) %reduce-scatter.8.cloned.1.call-update) | async-done | bytes 196624 | tf_op jit(solution)/shard_map/reduce_scatter | solution.py:257
  255.0 3.0 convolution_bitcast_fusion.2
  259.6 12.2 %fusion.70 = f32[2560,1280]{0,1:T(8,128)} fusion(f32[1280,2560]{1,0:T(8,128)} %fusion.98, bf16[768,1280]{0,1:T(8,128)(2,1)S(1)} %bitcast.368, bf16[768,2560]{1,0:T(8,128)(2,1)} %param.15), kind=kOutput, calls=%fused_computation.108 | convolution fusion | flops 5036441600 | bytes 32112640 | tf_op jit(solution)/shard_map/dot_general | solution.py:38
  271.7 14.0 %copy.180 = f32[2560,1280]{1,0:T(8,128)} copy(f32[2560,1280]{0,1:T(8,128)} %fusion.70) | data formatting | bytes 26214400
  287.3 2.2 multiply_reduce_fusion.1
  292.0 2.9 fusion.72
  298.1 22.0 %all-reduce = (f32[20]{0:T(128)S(1)}, f32[20]{0:T(128)}, f32[20]{0:T(128)}) all-reduce(f32[20]{0:T(128)S(1)} %get-tuple-element.482, f32[20]{0:T(128)S(1)} %get-tuple-element.481, f32[20]{0:T(128)S(1)} %reduce_sum.140), channel_id=1, replica_groups=mesh['seq'=8,'mp'=4] {'seq'}, use_global_device_ids=true, to_apply=%region_34.35 | all-reduce | flops 60 | bytes 480 | tf_op jit(solution)/shard_map/psum | solution.py:272
  320.7 4.3 reduce-scatter.12.cloned.1.call-done
  326.6 216.1 %reduce-scatter.10.cloned.1.call-done = f32[320,1280]{1,0:T(8,128)} async-done(((f32[2560,1280]{1,0:T(8,128)}), f32[320,1280]{1,0:T(8,128)}) %reduce-scatter.10.cloned.1.call-update) | async-done | bytes 1638416
  (394 shorter events, 108.8 us)
Async XLA Ops:
  7.2 154.0 %all-gather.6.cloned.1.call-start = ((), (), s32[]{:S(2)}) async-start(), calls=%async_computation.4 | async-start | bytes 5898240 | tf_op jit(solution)/shard_map/all_gather | solution.py:13
  8.9 3.2 copy-start.15
  42.0 175.1 %all-gather.4.cloned.1.call-start = ((), (), s32[]{:S(2)}) async-start(), calls=%async_computation.3 | async-start | bytes 5898240 | tf_op jit(solution)/shard_map/all_gather | solution.py:13
  42.7 212.2 %reduce-scatter.8.cloned.1.call-start = ((), (), s32[]{:S(2)}) async-start(), calls=%async_computation.5 | async-start | bytes 983040 | tf_op jit(solution)/shard_map/reduce_scatter | solution.py:257
  50.6 6.3 %copy-start.13 = (f32[3,256,20]{1,0,2:T(4,128)}, f32[3,256,20]{1,0,2:T(4,128)S(1)}, u32[]{:S(2)}) copy-start(f32[3,256,20]{1,0,2:T(4,128)S(1)} %get-tuple-element.820) | copy-start | bytes 184324 | tf_op jit(solution)/shard_map/while
  52.0 6.5 %copy-start.19 = (f32[1,256,20]{1,2,0:T(8,128)}, f32[1,256,20]{1,2,0:T(8,128)S(1)}, u32[]{:S(2)}) copy-start(f32[1,256,20]{1,2,0:T(8,128)S(1)} %copy.254) | copy-start | bytes 61444 | tf_op jit(solution)/shard_map/while
  52.0 6.5 %copy-start.21 = (f32[1,256,20]{1,2,0:T(8,128)}, f32[1,256,20]{1,2,0:T(8,128)S(1)}, u32[]{:S(2)}) copy-start(f32[1,256,20]{1,2,0:T(8,128)S(1)} %copy.255) | copy-start | bytes 61444 | tf_op jit(solution)/shard_map/while
  64.0 3.0 copy-start.20
  64.0 3.0 copy-start.22
  64.0 3.0 copy-start.29
  69.9 5.9 %copy-start.14 = (f32[3,256,20]{1,0,2:T(4,128)S(1)}, f32[3,256,20]{1,0,2:T(4,128)}, u32[]{:S(2)}) copy-start(f32[3,256,20]{1,0,2:T(4,128)} %copy-done.13) | copy-start | bytes 184324 | tf_op jit(solution)/shard_map/while
  75.9 6.1 %copy-start.13 = (f32[3,256,20]{1,0,2:T(4,128)}, f32[3,256,20]{1,0,2:T(4,128)S(1)}, u32[]{:S(2)}) copy-start(f32[3,256,20]{1,0,2:T(4,128)S(1)} %get-tuple-element.820) | copy-start | bytes 184324 | tf_op jit(solution)/shard_map/while
  77.3 6.5 %copy-start.19 = (f32[1,256,20]{1,2,0:T(8,128)}, f32[1,256,20]{1,2,0:T(8,128)S(1)}, u32[]{:S(2)}) copy-start(f32[1,256,20]{1,2,0:T(8,128)S(1)} %copy.254) | copy-start | bytes 61444 | tf_op jit(solution)/shard_map/while
  77.3 6.5 %copy-start.21 = (f32[1,256,20]{1,2,0:T(8,128)}, f32[1,256,20]{1,2,0:T(8,128)S(1)}, u32[]{:S(2)}) copy-start(f32[1,256,20]{1,2,0:T(8,128)S(1)} %copy.255) | copy-start | bytes 61444 | tf_op jit(solution)/shard_map/while
  89.3 3.0 copy-start.20
  95.3 5.9 %copy-start.14 = (f32[3,256,20]{1,0,2:T(4,128)S(1)}, f32[3,256,20]{1,0,2:T(4,128)}, u32[]{:S(2)}) copy-start(f32[3,256,20]{1,0,2:T(4,128)} %copy-done.13) | copy-start | bytes 184324 | tf_op jit(solution)/shard_map/while
  101.2 6.1 %copy-start.13 = (f32[3,256,20]{1,0,2:T(4,128)}, f32[3,256,20]{1,0,2:T(4,128)S(1)}, u32[]{:S(2)}) copy-start(f32[3,256,20]{1,0,2:T(4,128)S(1)} %get-tuple-element.820) | copy-start | bytes 184324 | tf_op jit(solution)/shard_map/while
  102.6 6.4 %copy-start.19 = (f32[1,256,20]{1,2,0:T(8,128)}, f32[1,256,20]{1,2,0:T(8,128)S(1)}, u32[]{:S(2)}) copy-start(f32[1,256,20]{1,2,0:T(8,128)S(1)} %copy.254) | copy-start | bytes 61444 | tf_op jit(solution)/shard_map/while
  102.6 6.4 %copy-start.21 = (f32[1,256,20]{1,2,0:T(8,128)}, f32[1,256,20]{1,2,0:T(8,128)S(1)}, u32[]{:S(2)}) copy-start(f32[1,256,20]{1,2,0:T(8,128)S(1)} %copy.255) | copy-start | bytes 61444 | tf_op jit(solution)/shard_map/while
  114.4 3.0 copy-start.20
  114.5 3.0 copy-start.22
  114.5 3.0 copy-start.29
  120.4 5.9 %copy-start.14 = (f32[3,256,20]{1,0,2:T(4,128)S(1)}, f32[3,256,20]{1,0,2:T(4,128)}, u32[]{:S(2)}) copy-start(f32[3,256,20]{1,0,2:T(4,128)} %copy-done.13) | copy-start | bytes 184324 | tf_op jit(solution)/shard_map/while
  126.3 4.4 copy-start.6
  228.6 3.3 copy-start
  233.4 91.5 %reduce-scatter.12.cloned.1.call-start = ((), (), s32[]{:S(2)}) async-start(), calls=%async_computation.7 | async-start | bytes 1474560
  239.2 8.4 %copy-start.1 = (f32[768,1280]{0,1:T(8,128)S(1)}, f32[768,1280]{0,1:T(8,128)}, u32[]{:S(2)}) copy-start(f32[768,1280]{0,1:T(8,128)} %copy.163) | copy-start | bytes 11796484
  239.2 8.4 %copy-start.25 = (f32[768,20]{0,1:T(8,128)S(1)}, f32[768,20]{0,1:T(8,128)}, u32[]{:S(2)}) copy-start(f32[768,20]{0,1:T(8,128)} %get-tuple-element.543) | copy-start | bytes 184324
  259.5 283.2 %reduce-scatter.10.cloned.1.call-start = ((), (), s32[]{:S(2)}) async-start(), calls=%async_computation.6 | async-start | bytes 14745600
  291.9 5.9 %copy-start.24 = (f32[768,20]{0,1:T(8,128)S(1)}, f32[768,20]{0,1:T(8,128)}, u32[]{:S(2)}) copy-start(f32[768,20]{0,1:T(8,128)} %param.19) | copy-start | bytes 184324
  292.0 5.9 %copy-start.28 = (f32[20]{0:T(128)S(1)}, f32[20]{0:T(128)}, u32[]{:S(2)}) copy-start(f32[20]{0:T(128)} %param.20) | copy-start | bytes 244
  294.8 25.3 %copy-start.30 = (f32[20]{0:T(128)S(1)}, f32[20]{0:T(128)}, u32[]{:S(2)}) copy-start(f32[20]{0:T(128)} %param.21) | copy-start | bytes 244
  (22 other events, 41.9 us)
Sparse Core Ops, SparseCore 0:
  42.1 88.6 all-gather.5
  132.9 84.0 all-gather.3
  233.5 21.3 reduce-scatter.7
  259.6 65.2 reduce-scatter.11
  329.0 213.6 reduce-scatter.9
where the time goes:
time: 553 us; the launch traced here: 549 us
  waiting for transfers between devices  272 us (49%)
  local copies, waits for them, and re-layouts  80.6 us (15%)
  matrix products  72.2 us (13%)
  other arithmetic  62.5 us (11%)
  blocking collectives  45 us (8%)
  between operations  14.4 us (3%)
    unnamed x7, waiting for transfers between devices  221 us
    all_gather x2, waiting for transfers between devices, entering(): everything = jax.tree.map(lambda part: lax.all_gather(part, axis), array)  45.6 us
    dot_general x16, matrix products, contract(): return jnp.einsum(form, left, right, preferred_element_type=jnp.float32)  34.3 us
    unnamed x60, local copies, waits for them, and re-layouts  31.6 us
    dot_general x6, matrix products, inner_first(): lax.dot_general(left, right, (((0,), (0,)), ((), ())), preferred_element_...  24.2 us
    all_gather x1, blocking collectives, entering(): everything = jax.tree.map(lambda part: lax.all_gather(part, axis), array)  22.9 us
    psum x1, blocking collectives, on_device(): lax.psum((stat_terms[0], stat_terms[1], stat_terms[2]), 'seq')  22 us
    select_n x16, other arithmetic, lap(): return jax.tree.map(lambda a, b: jnp.where(reached, a, b), new, before)  20 us
  transfers between devices with their start and end apart: 5, of which 4 were waited for; matrix products, arithmetic and copies ran while one was open for 28% of the time, Pallas kernels for 0%

commit v1 on v0

v1 whole, which is shorter than its diff:
```python
from functools import partial

import jax
import jax.numpy as jnp
from jax import lax
from jax.experimental import pallas as pl
from jax.experimental.pallas import tpu as pltpu
from jax.sharding import PartitionSpec as P

GROUP = 256
HALF = 128
ROWS = 16
LOG2E = 1.4426950408889634
HIGH = lax.Precision.HIGHEST
MESH = pl.DeviceIdType.MESH
F32 = jnp.float32
BF16 = jnp.bfloat16
L2, DT, EL, FE, SL, UPD, UPS, AFD, AFS, XB, YB = range(11)


def nn(a, b, precision=None):
    return lax.dot_general(
        a, b, (((1,), (0,)), ((), ())), precision=precision, preferred_element_type=F32
    )


def nt(a, b):
    return lax.dot_general(a, b, (((1,), (1,)), ((), ())), preferred_element_type=F32)


def tn(a, b):
    return lax.dot_general(a, b, (((0,), (0,)), ((), ())), preferred_element_type=F32)


def pair_wide(cols, row, first):
    low = cols[:, row : row + 1]
    high = cols[:, ROWS + row : ROWS + row + 1]
    return jnp.where(first, low, high)


def states_kernel(x_ref, dy_ref, b_ref, c_ref, tab_ref, s_ref, g_ref):
    cols = tab_ref[0].T
    first = lax.broadcasted_iota(jnp.int32, (1, 128), 1) < 64
    xb = (x_ref[...].astype(F32) * pair_wide(cols, XB, first)).astype(BF16)
    yb = (dy_ref[...].astype(F32) * pair_wide(cols, YB, first)).astype(BF16)
    s_ref[0] = tn(b_ref[...], xb)
    g_ref[0] = tn(c_ref[...], yb)


def group_kernel(
    groups, x_ref, dy_ref, b_ref, c_ref, tab_ref, skip_ref, sin_ref, gin_ref,
    dx_ref, dbc_ref, sums_ref, small_ref, cross, vt, starts, ends,
):
    pair = pl.program_id(0)
    state = b_ref.shape[1]
    first = lax.broadcasted_iota(jnp.int32, (1, 128), 1) < 64

    @pl.when(pair == 0)
    def _():
        row = lax.broadcasted_iota(jnp.int32, (GROUP, GROUP), 0)
        col = lax.broadcasted_iota(jnp.int32, (GROUP, GROUP), 1)
        for g in range(groups):
            at = pl.ds(g * GROUP, GROUP)
            both = nt(b_ref[at, :], c_ref[at, :])
            cross[at, :] = jnp.where(col >= row, both, 0.0)
        vt[...] = jnp.zeros_like(vt)
        dbc_ref[...] = jnp.zeros_like(dbc_ref)

    running = sin_ref[0]
    grads = []
    for g in range(groups):
        at = pl.ds(g * GROUP, GROUP)
        cols = tab_ref[0, :, at].T
        el = pair_wide(cols, EL, first)
        xw = x_ref[at, :].astype(F32) * (pair_wide(cols, DT, first) * pair_wide(cols, FE, first))
        yw = dy_ref[at, :].astype(F32) * el
        starts[g] = running
        decay = el[GROUP - 1 :, :]
        running = decay * running + tn(b_ref[at, :], xw.astype(BF16))
        grads.append((decay, tn(c_ref[at, :], yw.astype(BF16))))
    running = gin_ref[0]
    for g in range(groups - 1, -1, -1):
        ends[g] = running
        running = grads[g][0] * running + grads[g][1]

    for g in range(groups):
        at = pl.ds(g * GROUP, GROUP)
        tab = tab_ref[0, :, at]
        cols = tab.T
        el = pair_wide(cols, EL, first)
        fe = pair_wide(cols, FE, first)
        dt = pair_wide(cols, DT, first)
        x = x_ref[at, :]
        dy = dy_ref[at, :]
        xf = x.astype(F32)
        yf = dy.astype(F32)
        start = starts[g]
        end = ends[g]
        start_low = start.astype(BF16)
        end_low = end.astype(BF16)
        bg = b_ref[at, :]
        cg = c_ref[at, :]
        yw = yf * el
        xd = xf * dt
        g_end = nn(bg, end_low) * fe
        backward = yw * nn(cg, start_low)
        dbc_ref[at, :state] += nt((xd * fe).astype(BF16), end_low)
        dbc_ref[at, state:] += nt(yw.astype(BF16), start_low)
        intra = []
        for h in range(2):
            keep = first if h == 0 else jnp.logical_not(first)
            xm = jnp.where(keep, xf, 0.0).astype(BF16)
            l_row = tab[h * ROWS + L2 : h * ROWS + L2 + 1, :]
            parts = []
            col_sum = None
            weighted = None
            for a in range(GROUP // HALF):
                lo = a * HALF
                rows = slice(lo, lo + HALF)
                here = pl.ds(g * GROUP + lo, HALF)
                l_col = cols[rows, h * ROWS + L2 : h * ROWS + L2 + 1]
                dt_col = cols[rows, h * ROWS + DT : h * ROWS + DT + 1]
                q = jnp.exp2(jnp.minimum(l_row[:, lo:] - l_col, 0.0))
                cb = cross[here, lo:]
                mix = (cb * q).astype(BF16)
                parts.append(nn(mix, dy[lo:, :]))
                z = nt(xm[rows, :], dy[lo:, :]) * q * dt_col
                vt[here, lo:] += z
                box = cb * z
                down = jnp.sum(box, axis=0, keepdims=True)
                across = jnp.sum(box, axis=1, keepdims=True)
                row_w = jnp.sum(cols[rows, :] * across, axis=0, keepdims=True)
                if a == 0:
                    col_sum, weighted = down, row_w
                else:
                    col_sum = col_sum + jnp.concatenate(
                        [jnp.zeros((1, lo), F32), down], axis=1
                    )
                    weighted = weighted + row_w
            intra.append(jnp.concatenate(parts, axis=0))
            small_ref[0, g, h : h + 1, :] = col_sum
            small_ref[0, g, 2 + h : 3 + h, : 2 * ROWS] = weighted
        total = jnp.where(first, intra[0], intra[1]) + g_end
        dx_ref[at, :] = (dt * total + skip_ref[...] * yf).astype(BF16)
        products = jnp.concatenate([backward, xd * g_end, xf * total], axis=1)
        sums_ref[0, g] = nn(tab, products, HIGH)
        small_ref[0, g, 4:5, :128] = jnp.sum(start * end, axis=0, keepdims=True)
        small_ref[0, g, 5:6, :128] = jnp.sum(xf * yf, axis=0, keepdims=True)

    @pl.when(pair == pl.num_programs(0) - 1)
    def _():
        row = lax.broadcasted_iota(jnp.int32, (GROUP, GROUP), 0)
        col = lax.broadcasted_iota(jnp.int32, (GROUP, GROUP), 1)
        for g in range(groups):
            at = pl.ds(g * GROUP, GROUP)
            v = jnp.where(col >= row, vt[at, :], 0.0).astype(BF16)
            dbc_ref[at, :state] += nn(v, c_ref[at, :])
            dbc_ref[at, state:] += tn(v, b_ref[at, :])


def chain_kernel(n, s_ref, g_ref, e_ref, sin_ref, gin_ref, s_in, g_in, s_out, g_out,
                 s_send, s_recv, g_send, g_recv):
    me = lax.axis_index("seq")
    chunks = s_ref.shape[0]
    up = lax.rem(me + 1, n)
    down = lax.rem(me + n - 1, n)
    barrier = pltpu.get_barrier_semaphore()
    for other in (up, down):
        pl.semaphore_signal(barrier, inc=1, device_id={"seq": other}, device_id_type=MESH)
    pl.semaphore_wait(barrier, 2)

    def copy(c, out, into, send, recv, target):
        return pltpu.make_async_remote_copy(
            src_ref=out.at[c], dst_ref=into.at[c], send_sem=send.at[c], recv_sem=recv.at[c],
            device_id={"seq": target}, device_id_type=MESH,
        )

    def hop(c, hops, own, result, out, into, send, recv, target):
        @pl.when(hops == 0)
        def _():
            result[c] = jnp.zeros(result.shape[1:], F32)

        @pl.when(hops > 0)
        def _():
            copy(c, out, into, send, recv, target).wait_recv()
            result[c] = into[c]

        @pl.when(hops < n - 1)
        def _():
            out[c] = e_ref[c, :1, :] * result[c] + own[c]
            copy(c, out, into, send, recv, target).start()

    lag = 2

    def slot(k, carry):
        c = k - lag * me

        @pl.when(jnp.logical_and(c >= 0, c < chunks))
        def _():
            hop(c, me, s_ref, sin_ref, s_out, s_in, s_send, s_recv, up)

        far = n - 1 - me
        d = k - lag * far

        @pl.when(jnp.logical_and(d >= 0, d < chunks))
        def _():
            hop(d, far, g_ref, gin_ref, g_out, g_in, g_send, g_recv, down)

        return carry

    lax.fori_loop(0, lag * (n - 1) + chunks, slot, 0)

    @pl.when(me < n - 1)
    def _():
        for c in range(chunks):
            copy(c, s_out, s_in, s_send, s_recv, up).wait_send()

    @pl.when(me > 0)
    def _():
        for c in range(chunks):
            copy(c, g_out, g_in, g_send, g_recv, down).wait_send()


def ring_place(i, n):
    if n % 2:
        return lax.rem(i + n, n)
    return jnp.where(lax.rem(i, 2) == 0, lax.div(i, 2), n - 1 - lax.div(i, 2))


def ring_index(p, n):
    p = lax.rem(p + 2 * n, n)
    if n % 2:
        return p
    return jnp.where(p < n // 2, 2 * p, 2 * (n - 1 - p) + 1)


def ring_kernel(n, q, lt_ref, dx_ref, st_ref, out_ref, sto_ref, slots, peers,
                send, recv, st_send, st_recv):
    me = lax.axis_index("seq")
    p = ring_place(me, n)
    targets = (ring_index(p + 1, n), ring_index(p - 1, n))
    half = slots.shape[3]
    width = slots.shape[4]
    barrier = pltpu.get_barrier_semaphore()
    for j in range(1, n):
        pl.semaphore_signal(
            barrier, inc=1, device_id={"seq": lax.rem(me + j, n)}, device_id_type=MESH
        )
    pl.semaphore_wait(barrier, n - 1)

    def own(s, d, k):
        block = ring_index(p - 1 - s, n) if d == 0 else ring_index(p + 1 + s, n)
        return nn(lt_ref[2 * block + d], dx_ref[:, k * width : (k + 1) * width])

    def copy(s, d, k):
        return pltpu.make_async_remote_copy(
            src_ref=slots.at[s, d, k], dst_ref=slots.at[s + 1, d, k],
            send_sem=send.at[s, d, k], recv_sem=recv.at[s + 1, d, k],
            device_id={"seq": targets[d]}, device_id_type=MESH,
        )

    def stat(j):
        return pltpu.make_async_remote_copy(
            src_ref=st_ref, dst_ref=peers.at[j], send_sem=st_send.at[j], recv_sem=st_recv.at[j],
            device_id={"seq": lax.rem(me + j, n)}, device_id_type=MESH,
        )

    for k in range(q):
        for d in range(2):
            slots[0, d, k] = own(0, d, k)
            copy(0, d, k).start()
    for j in range(1, n):
        stat(j).start()

    def step(s, carry):
        for k in range(q):
            for d in range(2):
                mine = own(s, d, k)
                copy(s - 1, d, k).wait_recv()
                slots[s, d, k] = slots[s, d, k] + mine
                copy(s, d, k).start()
        return carry

    lax.fori_loop(1, n - 1, step, 0)
    for k in range(q):
        for d in range(2):
            mine = own(n - 1, d, k)
            copy(n - 2, d, k).wait_recv()
            out_ref[d * half : (d + 1) * half, k * width : (k + 1) * width] = (
                slots[n - 1, d, k] + mine
            )
    total = st_ref[...]
    for j in range(1, n):
        stat(j).wait_recv()
        total = total + peers[j]
    sto_ref[...] = total

    def drain(s, carry):
        for k in range(q):
            for d in range(2):
                copy(s, d, k).wait_send()
        return carry

    lax.fori_loop(0, n - 1, drain, 0)
    for j in range(1, n):
        stat(j).wait_send()


def vmem(count):
    return [pl.BlockSpec(memory_space=pltpu.VMEM)] * count


def on_device(layer_in, ssm_input, b_matrix, c_matrix, dt_raw, dt_bias, a_log, d_skip, grad_out):
    n = lax.axis_size("seq")
    tok, heads = dt_raw.shape
    width = ssm_input.shape[1]
    dim = width // heads
    state = b_matrix.shape[1]
    groups = tok // GROUP
    pairs = heads // 2
    depth = layer_in.shape[1]

    shifted = dt_raw.T + dt_bias[:, None]
    dt = jax.nn.softplus(shifted)
    slope = jax.nn.sigmoid(shifted)
    rate = -jnp.exp(a_log)
    step = dt * rate[:, None]
    stacked = jnp.stack([step, dt, slope]).reshape(3, heads, groups, GROUP)
    tri = jnp.triu(jnp.ones((GROUP, GROUP), F32))
    sums = lax.dot_general(
        stacked, tri, (((3,), (0,)), ((), ())), precision=HIGH, preferred_element_type=F32
    )
    within, up_dt, up_sl = sums[0], sums[1], sums[2]
    last = sums[..., -1:]
    lend = within[..., -1:]
    offset = jnp.cumsum(lend, axis=1) - lend
    bend = jnp.sum(lend, axis=1, keepdims=True)
    cumulative = within + offset
    after = last[1:] - sums[1:]
    fall = jnp.exp(lend - within)
    dt3 = dt.reshape(heads, groups, GROUP)
    rows = [
        within * LOG2E, dt3, jnp.exp(within), fall, slope.reshape(heads, groups, GROUP),
        up_dt, up_sl, after[0], after[1], dt3 * jnp.exp(bend - cumulative), jnp.exp(cumulative),
    ]
    rows = rows + [jnp.zeros_like(within)] * (ROWS - len(rows))
    table = jnp.stack(rows, axis=1).reshape(pairs, 2 * ROWS, tok)

    wide = pl.BlockSpec((tok, 2 * dim), lambda i: (0, i))
    whole = pl.BlockSpec((tok, state), lambda i: (0, 0))
    tab_spec = pl.BlockSpec((1, 2 * ROWS, tok), lambda i: (i, 0, 0))
    square = pl.BlockSpec((1, state, 2 * dim), lambda i: (i, 0, 0))
    states = jax.ShapeDtypeStruct((pairs, state, 2 * dim), F32)
    block_state, block_grad = pl.pallas_call(
        states_kernel,
        grid=(pairs,),
        in_specs=[wide, wide, whole, whole, tab_spec],
        out_specs=[square, square],
        out_shape=[states, states],
        name="block_states",
    )(ssm_input, grad_out, b_matrix, c_matrix, table)

    decay = jnp.repeat(jnp.exp(bend[:, 0, 0]), dim).reshape(pairs, 1, 2 * dim)
    decay = jnp.broadcast_to(decay, (pairs, 8, 2 * dim))
    buffers = pltpu.VMEM((pairs, state, 2 * dim), F32)
    sems = pltpu.SemaphoreType.DMA((pairs,))
    state_in, grad_in = pl.pallas_call(
        partial(chain_kernel, n),
        in_specs=vmem(3),
        out_specs=vmem(2),
        out_shape=[states, states],
        scratch_shapes=[buffers] * 4 + [sems] * 4,
        compiler_params=pltpu.CompilerParams(collective_id=1, has_side_effects=True),
        name="state_chain",
    )(block_state, block_grad, decay)

    skip_row = jnp.repeat(d_skip, dim).reshape(1, width)
    dx, dbc, weighted, small = pl.pallas_call(
        partial(group_kernel, groups),
        grid=(pairs,),
        in_specs=[
            wide, wide, whole, whole, tab_spec,
            pl.BlockSpec((1, 2 * dim), lambda i: (0, i)), square, square,
        ],
        out_specs=[
            wide,
            pl.BlockSpec((tok, 2 * state), lambda i: (0, 0)),
            pl.BlockSpec((1, groups, 2 * ROWS, 6 * dim), lambda i: (i, 0, 0, 0)),
            pl.BlockSpec((1, groups, 8, GROUP), lambda i: (i, 0, 0, 0)),
        ],
        out_shape=[
            jax.ShapeDtypeStruct((tok, width), BF16),
            jax.ShapeDtypeStruct((tok, 2 * state), F32),
            jax.ShapeDtypeStruct((pairs, groups, 2 * ROWS, 6 * dim), F32),
            jax.ShapeDtypeStruct((pairs, groups, 8, GROUP), F32),
        ],
        scratch_shapes=[
            pltpu.VMEM((tok, GROUP), F32),
            pltpu.VMEM((tok, GROUP), F32),
            pltpu.VMEM((groups, state, 2 * dim), F32),
            pltpu.VMEM((groups, state, 2 * dim), F32),
        ],
        name="group_terms",
    )(ssm_input, grad_out, b_matrix, c_matrix, table, skip_row, state_in, grad_in)

    owned = lax.psum_scatter(dbc, "mp", scatter_dimension=1, tiled=True).astype(BF16)
    grad_wbc = lax.psum_scatter(
        lax.dot_general(
            layer_in, owned, (((0,), (0,)), ((), ())), preferred_element_type=F32
        ),
        "seq", scatter_dimension=0, tiled=True,
    )

    folded = jnp.sum(
        weighted.reshape(pairs, groups, 2, ROWS, 3, 2, dim), axis=(1, 6)
    )
    own = jnp.stack([folded[:, 0, :, :, 0], folded[:, 1, :, :, 1]], axis=1)
    own = own.reshape(heads, ROWS, 3)
    row_w = jnp.stack(
        [small[:, :, 2, :ROWS], small[:, :, 3, ROWS : 2 * ROWS]], axis=1
    ).sum(axis=2).reshape(heads, ROWS)
    col_sum = jnp.swapaxes(small[:, :, :2, :], 1, 2).reshape(heads, groups, GROUP)
    meet = small[:, :, 4, : 2 * dim].reshape(pairs, groups, 2, dim).sum(axis=3)
    meet = jnp.swapaxes(meet, 1, 2).reshape(heads, groups) * jnp.exp(lend[..., 0])
    skip_sum = small[:, :, 5, : 2 * dim].reshape(pairs, groups, 2, dim).sum(axis=(1, 3))

    def through(ups, up_row, after_row, k):
        return (
            own[:, up_row, 0] + own[:, after_row, 1]
            + jnp.sum(ups * col_sum, axis=(1, 2)) - row_w[:, up_row]
            + jnp.sum(meet * last[k, :, :, 0], axis=1)
        )

    rate_part = through(up_dt, UPD, AFD, 1)
    bias_part = own[:, SL, 2] + rate * through(up_sl, UPS, AFS, 2)
    stat = jnp.zeros((8, 128), F32)
    stat = stat.at[:3, :heads].set(
        jnp.stack([rate_part, bias_part, skip_sum.reshape(heads)])
    )

    block = depth // n
    half = block // 2
    q = 2
    lt = layer_in.T.reshape(2 * n, half, tok)
    ring = pltpu.SemaphoreType.DMA((n, 2, q))
    each = pltpu.SemaphoreType.DMA((n,))
    grad_wx, totals = pl.pallas_call(
        partial(ring_kernel, n, q),
        in_specs=vmem(3),
        out_specs=vmem(2),
        out_shape=[
            jax.ShapeDtypeStruct((block, width), F32),
            jax.ShapeDtypeStruct((8, 128), F32),
        ],
        scratch_shapes=[
            pltpu.VMEM((n, 2, q, half, width // q), F32),
            pltpu.VMEM((n, 8, 128), F32),
            ring, ring, each, each,
        ],
        compiler_params=pltpu.CompilerParams(collective_id=2, has_side_effects=True),
        cost_estimate=pl.CostEstimate(
            flops=60 * 2 * tok * depth * width, bytes_accessed=2 * depth * width, transcendentals=0
        ),
        name="ring_projection",
    )(lt, dx, stat)
    return (
        grad_wx, grad_wbc, rate * totals[0, :heads], totals[1, :heads], totals[2, :heads],
    )


def solution(mesh):
    in_specs = (
        P("seq", None),
        P("seq", "mp"),
        P("seq", None),
        P("seq", None),
        P("seq", "mp"),
        P("mp"),
        P("mp"),
        P("mp"),
        P("seq", "mp"),
    )
    out_specs = (P("seq", "mp"), P("seq", "mp"), P("mp"), P("mp"), P("mp"))
    return jax.shard_map(
        on_device, mesh=mesh, in_specs=in_specs, out_specs=out_specs, check_vma=False
    )
```

time: 553 us -> 317 us (0.57)
  waiting for transfers between devices: 272 us -> 9.62 us
  Pallas kernels: 0 us -> 259 us
  matrix products: 72.2 us -> 3.38 us
  local copies, waits for them, and re-layouts: 80.6 us -> 23.5 us
  other arithmetic: 62.5 us -> 6.39 us
  blocking collectives: 45 us -> 0 us
    pallas_call x0 -> x4, Pallas kernels: none -> 259 us  [the longest x1 150 us: on_device(): pl.pallas_call(partial(ring_kernel, n, q), in_specs=vmem(3), out_specs=vm...]
    unnamed x7 -> x4, waiting for transfers between devices: 221 us -> 9.62 us
    dot_general x36 -> x2, matrix products: 72.2 us -> 3.38 us  [the longest x1 2.95 us: on_device(): lax.dot_general(layer_in, owned, (((0,), (0,)), ((), ())), preferred_elem...]
    all_gather x2 -> x0, waiting for transfers between devices: 45.6 us -> none  [entering(): everything = jax.tree.map(lambda part: lax.all_gather(part, axis), array)]
    all_gather x1 -> x0, blocking collectives: 22.9 us -> none  [entering(): everything = jax.tree.map(lambda part: lax.all_gather(part, axis), array)]
    psum x1 -> x0, blocking collectives: 22 us -> none  [on_device(): lax.psum((stat_terms[0], stat_terms[1], stat_terms[2]), 'seq')]
    unnamed x60 -> x29, local copies, waits for them, and re-layouts: 31.6 us -> 10.3 us
    select_n x16 -> x0, other arithmetic: 20 us -> none  [lap(): return jax.tree.map(lambda a, b: jnp.where(reached, a, b), new, before)]
  transfers between devices with their start and end apart: 5 -> 2, of which waited for: 4 -> 1; matrix products, arithmetic and copies ran while one was open for 28% -> 4% of each run, Pallas kernels for 0% -> 47%
where the time goes in v1:
time: 317 us
  Pallas kernels  259 us (82%)
  local copies, waits for them, and re-layouts  23.5 us (7%)
  between operations  14.4 us (5%)
  waiting for transfers between devices  9.62 us (3%)
  other arithmetic  6.39 us (2%)
  matrix products  3.38 us (1%)
    pallas_call x1, Pallas kernels, on_device(): pl.pallas_call(partial(ring_kernel, n, q), in_specs=vmem(3), out_specs=vm...  150 us
    pallas_call x1, Pallas kernels, on_device(): pl.pallas_call(partial(chain_kernel, n), in_specs=vmem(3), out_specs=vmem...  57.1 us
    pallas_call x1, Pallas kernels, on_device(): pl.pallas_call(partial(group_kernel, groups), grid=(pairs,), in_specs=[wi...  40.3 us
    pallas_call x1, Pallas kernels, on_device(): pl.pallas_call(states_kernel, grid=(pairs,), in_specs=[wide, wide, whole,...  11.8 us
    unnamed x29, local copies, waits for them, and re-layouts  10.3 us
    unnamed x4, waiting for transfers between devices  9.62 us
  transfers between devices with their start and end apart: 2, of which 1 were waited for; matrix products, arithmetic and copies ran while one was open for 4% of the time, Pallas kernels for 47%

profile of v1, /device:TPU:0, one launch (start us, length us, event | category | flops | bytes accessed | tf_op | source)
XLA Modules:
  0.0 316.5 jit_solution(5338399814800318270)
XLA Ops:
  7.2 0.7 exponential_negate_fusion
  7.9 1.0 broadcast_multiply_fusion
  9.2 0.4 fusion
  9.7 0.2 fusion.31
  9.9 0.2 slice_reduce_fusion.2
  10.2 0.7 reshape_reshape.4.skip_ref
  12.1 1.6 reshape.194.tab_ref
  13.7 11.8 %block_states.1 = (f32[10,128,128]{2,1,0:T(8,128)}, f32[10,128,128]{2,1,0:T(8,128)}) custom-call(bf16[768,1280]{1,0:T(8,128)(2,1)} %x_ref.3, bf16[768,1280]{1,0:T(8,128)(2,1)} %dy_ref.3, bf16[768,128]{1,0:T(8,128)(2,1)} %b_ref.3, bf16[768,128]{1,0:T(8,128)(2,1)} %c_ref.3, f32[10,32,768]{2,1,0:T(8,128)} %reshape.194.tab_ref), custom_call_target="tpu_custom_call" | custom-call | tf_op jit(solution)/shard_map/block_states/pallas_call | solution.py:354
  25.5 0.6 broadcast_in_dim.29.e_ref
  26.2 57.1 %state_chain.1 = (f32[10,128,128]{2,1,0:T(8,128)}, f32[10,128,128]{2,1,0:T(8,128)}) custom-call(f32[10,128,128]{2,1,0:T(8,128)} %get-tuple-element.27.s_ref, f32[10,128,128]{2,1,0:T(8,128)} %get-tuple-element.28.g_ref, f32[10,8,128]{2,1,0:T(8,128)} %broadcast_in_dim.29.e_ref), custom_call_target="tpu_custom_call" | custom-call | tf_op jit(solution)/shard_map/state_chain/pallas_call | solution.py:367
  83.3 40.3 %group_terms.1 = (bf16[768,1280]{1,0:T(8,128)(2,1)}, f32[768,256]{1,0:T(8,128)}, f32[10,3,32,384]{3,2,1,0:T(8,128)}, f32[10,3,8,256]{3,2,1,0:T(8,128)}) custom-call(bf16[768,1280]{1,0:T(8,128)(2,1)} %x_ref.3, bf16[768,1280]{1,0:T(8,128)(2,1)} %dy_ref.3, bf16[768,128]{1,0:T(8,128)(2,1)} %b_ref.3, bf16[768,128]{1,0:T(8,128)(2,1)} %c_ref.3, ...), custom_call_target="tpu_custom_call" | custom-call | tf_op jit(solution)/shard_map/group_terms/pallas_call | solution.py:378
  123.6 2.4 copy.141
  126.0 0.2 reduce-scatter.9.cloned.1.call-start
  127.4 0.6 reduce_sum.101
  128.0 1.4 reduce_sum.102
  129.4 0.2 fusion.30
  129.6 0.2 copy.147
  129.8 0.3 copy.148
  130.2 6.3 %copy.116 = bf16[2560,768]{1,0:T(8,128)(2,1)} copy(bf16[2560,768]{0,1:T(8,128)(2,1)} %bitcast.107) | data formatting | bytes 7864320 | tf_op jit(solution)/shard_map/transpose | solution.py:444
  136.6 0.2 slice_reduce_fusion.1
  136.8 0.2 slice_reduce_fusion.8
  137.0 0.2 fusion.25
  137.4 0.6 select_maximum_fusion.st_ref
  138.0 9.6 %reduce-scatter.7.cloned.1.call-done = f32[64,768]{1,0:T(8,128)} async-done(((f32[256,768]{1,0:T(8,128)}), f32[64,768]{1,0:T(8,128)}) %reduce-scatter.7.cloned.1.call-update) | async-done | bytes 196624
  147.5 1.1 copy.142
  148.6 2.9 convolution_bitcast_fusion
  151.6 1.5 copy.143
  153.1 149.7 %ring_projection.1 = (f32[320,1280]{1,0:T(8,128)}, f32[8,128]{1,0:T(8,128)}) custom-call(bf16[16,160,768]{2,1,0:T(8,128)(2,1)} %bitcast.108, bf16[768,1280]{1,0:T(8,128)(2,1)} %get-tuple-element.31.dx_ref, f32[8,128]{1,0:T(8,128)} %select_maximum_fusion.st_ref), custom_call_target="tpu_custom_call" | custom-call | flops 301989888000 | bytes 6553600 | tf_op jit(solution)/shard_map/ring_projection/pallas_call | solution.py:447
  302.9 1.2 bitcast_multiply_fusion.3
  304.0 1.3 slice_bitcast_fusion.8
  305.3 1.7 copy.144
  307.0 2.7 copy.172
  (70 shorter events, 2.9 us)
Async XLA Ops:
  7.2 140.4 %reduce-scatter.7.cloned.1.call-start = ((), (), s32[]{:S(2)}) async-start(), calls=%async_computation.2 | async-start | bytes 983040
  7.9 2.2 copy-start.2
  123.6 2.7 copy-start.1
  123.6 3.6 %copy-start = (f32[10,3,32,384]{3,2,1,0:T(8,128)S(1)}, f32[10,3,32,384]{3,2,1,0:T(8,128)}, u32[]{:S(2)}) copy-start(f32[10,3,32,384]{3,2,1,0:T(8,128)} %get-tuple-element.32) | copy-start | bytes 4423684
  126.0 179.3 %reduce-scatter.9.cloned.1.call-start = ((), (), s32[]{:S(2)}) async-start(), calls=%async_computation.3 | async-start | bytes 1474560
  130.2 7.1 %copy-start.3 = (f32[20]{0:T(128)S(1)}, f32[20]{0:T(128)}, u32[]{:S(2)}) copy-start(f32[20]{0:T(128)} %param.17) | copy-start | bytes 244
  153.1 149.8 %copy-start.4 = (f32[20]{0:T(128)S(1)}, f32[20]{0:T(128)}, u32[]{:S(2)}) copy-start(f32[20]{0:T(128)} %param.17) | copy-start | bytes 244
Sparse Core Ops, SparseCore 0:
  126.2 21.3 reduce-scatter.6
  153.2 70.6 reduce-scatter.8

commit v2 on v1

--- a/solution.py
+++ b/solution.py
@@ -48,8 +48,8 @@
 
 
 def group_kernel(
-    groups, x_ref, dy_ref, b_ref, c_ref, tab_ref, skip_ref, sin_ref, gin_ref,
-    dx_ref, dbc_ref, sums_ref, small_ref, cross, vt, starts, ends,
+    groups, x_ref, dy_ref, b_ref, c_ref, tab_ref, skip_ref, sin_ref, gin_ref, layer_ref,
+    dx_ref, out_ref, sums_ref, small_ref, turned_ref, cross, vt, starts, ends, dbc_ref,
 ):
     pair = pl.program_id(0)
     state = b_ref.shape[1]
@@ -66,6 +66,7 @@
         vt[...] = jnp.zeros_like(vt)
         dbc_ref[...] = jnp.zeros_like(dbc_ref)
 
+    turned_ref[...] = layer_ref[...].T
     running = sin_ref[0]
     grads = []
     for g in range(groups):
@@ -156,69 +157,107 @@
             v = jnp.where(col >= row, vt[at, :], 0.0).astype(BF16)
             dbc_ref[at, :state] += nn(v, c_ref[at, :])
             dbc_ref[at, state:] += tn(v, b_ref[at, :])
-
-
-def chain_kernel(n, s_ref, g_ref, e_ref, sin_ref, gin_ref, s_in, g_in, s_out, g_out,
-                 s_send, s_recv, g_send, g_recv):
+        out_ref[...] = dbc_ref[...].T
+
+
+def chain_kernel(n, s_ref, g_ref, e_ref, sin_ref, gin_ref, mate, mate_e, passed, lent, made,
+                 mate_send, mate_recv, e_sem, pass_send, pass_recv, lend_send, lend_recv):
     me = lax.axis_index("seq")
     chunks = s_ref.shape[0]
-    up = lax.rem(me + 1, n)
-    down = lax.rem(me + n - 1, n)
+    steps = n // 2
+    odd = lax.rem(me, 2)
+    place = lax.div(me, 2)
+    partner = me + 1 - 2 * odd
+    up = lax.rem(me + 2, n)
+    down = lax.rem(me + n - 2, n)
     barrier = pltpu.get_barrier_semaphore()
-    for other in (up, down):
+    for other in (partner, up, down):
         pl.semaphore_signal(barrier, inc=1, device_id={"seq": other}, device_id_type=MESH)
-    pl.semaphore_wait(barrier, 2)
-
-    def copy(c, out, into, send, recv, target):
+    pl.semaphore_wait(barrier, 3)
+
+    def remote(src, dst, send, recv, target):
         return pltpu.make_async_remote_copy(
-            src_ref=out.at[c], dst_ref=into.at[c], send_sem=send.at[c], recv_sem=recv.at[c],
+            src_ref=src, dst_ref=dst, send_sem=send, recv_sem=recv,
             device_id={"seq": target}, device_id_type=MESH,
         )
 
-    def hop(c, hops, own, result, out, into, send, recv, target):
-        @pl.when(hops == 0)
+    def run(tail_own, tail_in, tail_hops, target, head_own, head_in):
+        head_hops = steps - 1 - tail_hops
+
+        def to_mate(c):
+            return remote(head_own.at[c], mate.at[c], mate_send.at[c], mate_recv.at[c], partner)
+
+        def onward(c):
+            return remote(made.at[c], passed.at[c], pass_send.at[c], pass_recv.at[c], target)
+
+        def aside(c):
+            return remote(passed.at[c], lent.at[c], lend_send.at[c], lend_recv.at[c], partner)
+
+        decay = remote(e_ref, mate_e, e_sem.at[0], e_sem.at[1], partner)
+        decay.start()
+        for c in range(chunks):
+            to_mate(c).start()
+        decay.wait_recv()
+        lag = 2
+
+        def slot(k, carry):
+            c = k - lag * tail_hops
+            d = k - lag * head_hops - 2
+
+            @pl.when(jnp.logical_and(c >= 0, c < chunks))
+            def _():
+                to_mate(c).wait_recv()
+
+                @pl.when(tail_hops == 0)
+                def _():
+                    tail_in[c] = mate[c]
+
+                @pl.when(tail_hops > 0)
+                def _():
+                    onward(c).wait_recv()
+                    aside(c).start()
+                    tail_in[c] = mate_e[c, :1, :] * passed[c] + mate[c]
+
+                @pl.when(tail_hops < steps - 1)
+                def _():
+                    made[c] = e_ref[c, :1, :] * tail_in[c] + tail_own[c]
+                    onward(c).start()
+
+            @pl.when(jnp.logical_and(d >= 0, d < chunks))
+            def _():
+                @pl.when(head_hops == 0)
+                def _():
+                    head_in[d] = jnp.zeros(head_in.shape[1:], F32)
+
+                @pl.when(head_hops > 0)
+                def _():
+                    aside(d).wait_recv()
+                    head_in[d] = lent[d]
+
+            return carry
+
+        lax.fori_loop(0, lag * (steps - 1) + chunks + 2, slot, 0)
+        decay.wait_send()
+        for c in range(chunks):
+            to_mate(c).wait_send()
+
+        @pl.when(tail_hops > 0)
         def _():
-            result[c] = jnp.zeros(result.shape[1:], F32)
-
-        @pl.when(hops > 0)
+            for c in range(chunks):
+                aside(c).wait_send()
+
+        @pl.when(tail_hops < steps - 1)
         def _():
-            copy(c, out, into, send, recv, target).wait_recv()
-            result[c] = into[c]
-
-        @pl.when(hops < n - 1)
-        def _():
-            out[c] = e_ref[c, :1, :] * result[c] + own[c]
-            copy(c, out, into, send, recv, target).start()
-
-    lag = 2
-
-    def slot(k, carry):
-        c = k - lag * me
-
-        @pl.when(jnp.logical_and(c >= 0, c < chunks))
-        def _():
-            hop(c, me, s_ref, sin_ref, s_out, s_in, s_send, s_recv, up)
-
-        far = n - 1 - me
-        d = k - lag * far
-
-        @pl.when(jnp.logical_and(d >= 0, d < chunks))
-        def _():
-            hop(d, far, g_ref, gin_ref, g_out, g_in, g_send, g_recv, down)
-
-        return carry
-
-    lax.fori_loop(0, lag * (n - 1) + chunks, slot, 0)
-
-    @pl.when(me < n - 1)
+            for c in range(chunks):
+                onward(c).wait_send()
+
+    @pl.when(odd == 1)
     def _():
-        for c in range(chunks):
-            copy(c, s_out, s_in, s_send, s_recv, up).wait_send()
-
-    @pl.when(me > 0)
+        run(s_ref, sin_ref, place, up, g_ref, gin_ref)
+
+    @pl.when(odd == 0)
     def _():
-        for c in range(chunks):
-            copy(c, g_out, g_in, g_send, g_recv, down).wait_send()
+        run(g_ref, gin_ref, steps - 1 - place, down, s_ref, sin_ref)
 
 
 def ring_place(i, n):
@@ -234,9 +273,11 @@
     return jnp.where(p < n // 2, 2 * p, 2 * (n - 1 - p) + 1)
 
 
-def ring_kernel(n, q, lt_ref, dx_ref, st_ref, out_ref, sto_ref, slots, peers,
-                send, recv, st_send, st_recv):
+def ring_kernel(n, m, q, lt_ref, dx_ref, bc_ref, st_ref, out_ref, wbc_ref, sto_ref,
+                slots, narrow, low, others, peers,
+                send, recv, n_send, n_recv, o_send, o_recv, st_send, st_recv):
     me = lax.axis_index("seq")
+    mine_mp = lax.axis_index("mp")
     p = ring_place(me, n)
     targets = (ring_index(p + 1, n), ring_index(p - 1, n))
     half = slots.shape[3]
@@ -246,7 +287,36 @@
         pl.semaphore_signal(
             barrier, inc=1, device_id={"seq": lax.rem(me + j, n)}, device_id_type=MESH
         )
-    pl.semaphore_wait(barrier, n - 1)
+    for j in range(1, m):
+        pl.semaphore_signal(
+            barrier, inc=1, device_id={"mp": lax.rem(mine_mp + j, m)}, device_id_type=MESH
+        )
+    pl.semaphore_wait(barrier, n + m - 2)
+    cols = low.shape[0]
+    quarter = half // 2
+
+    def own_narrow(s, d):
+        block = ring_index(p - 1 - s, n) if d == 0 else ring_index(p + 1 + s, n)
+        both = nt(lt_ref[2 * block + d], low[...])
+        return jnp.concatenate([both[:quarter], both[quarter:]], axis=1)
+
+    def copy_narrow(s, d):
+        return pltpu.make_async_remote_copy(
+            src_ref=narrow.at[s, d], dst_ref=narrow.at[s + 1, d],
+            send_sem=n_send.at[s, d], recv_sem=n_recv.at[s + 1, d],
+            device_id={"seq": targets[d]}, device_id_type=MESH,
+        )
+
+    def other(j):
+        at = lax.rem(mine_mp + j, m)
+        return pltpu.make_async_remote_copy(
+            src_ref=bc_ref.at[at], dst_ref=others.at[j],
+            send_sem=o_send.at[j], recv_sem=o_recv.at[j],
+            device_id={"mp": at}, device_id_type=MESH,
+        )
+
+    for j in range(1, m):
+        other(j).start()
 
     def own(s, d, k):
         block = ring_index(p - 1 - s, n) if d == 0 else ring_index(p + 1 + s, n)
@@ -271,6 +341,14 @@
             copy(0, d, k).start()
     for j in range(1, n):
         stat(j).start()
+    summed = bc_ref[mine_mp]
+    for j in range(1, m):
+        other(j).wait_recv()
+        summed = summed + others[j]
+    low[...] = summed.astype(BF16)
+    for d in range(2):
+        narrow[0, d] = own_narrow(0, d)
+        copy_narrow(0, d).start()
 
     def step(s, carry):
         for k in range(q):
@@ -279,6 +357,11 @@
                 copy(s - 1, d, k).wait_recv()
                 slots[s, d, k] = slots[s, d, k] + mine
                 copy(s, d, k).start()
+        for d in range(2):
+            mine = own_narrow(s, d)
+            copy_narrow(s - 1, d).wait_recv()
+            narrow[s, d] = narrow[s, d] + mine
+            copy_narrow(s, d).start()
         return carry
 
     lax.fori_loop(1, n - 1, step, 0)
@@ -289,6 +372,12 @@
             out_ref[d * half : (d + 1) * half, k * width : (k + 1) * width] = (
                 slots[n - 1, d, k] + mine
             )
+    for d in range(2):
+        mine = own_narrow(n - 1, d)
+        copy_narrow(n - 2, d).wait_recv()
+        both = narrow[n - 1, d] + mine
+        wbc_ref[d * half : d * half + quarter, :] = both[:, :cols]
+        wbc_ref[d * half + quarter : (d + 1) * half, :] = both[:, cols:]
     total = st_ref[...]
     for j in range(1, n):
         stat(j).wait_recv()
@@ -299,11 +388,15 @@
         for k in range(q):
             for d in range(2):
                 copy(s, d, k).wait_send()
+        for d in range(2):
+            copy_narrow(s, d).wait_send()
         return carry
 
     lax.fori_loop(0, n - 1, drain, 0)
     for j in range(1, n):
         stat(j).wait_send()
+    for j in range(1, m):
+        other(j).wait_send()
 
 
 def vmem(count):
@@ -335,13 +428,14 @@
     lend = within[..., -1:]
     offset = jnp.cumsum(lend, axis=1) - lend
     bend = jnp.sum(lend, axis=1, keepdims=True)
+    later = jnp.exp(jnp.minimum(bend - offset - lend, 0.0))
     cumulative = within + offset
     after = last[1:] - sums[1:]
     fall = jnp.exp(lend - within)
     dt3 = dt.reshape(heads, groups, GROUP)
     rows = [
         within * LOG2E, dt3, jnp.exp(within), fall, slope.reshape(heads, groups, GROUP),
-        up_dt, up_sl, after[0], after[1], dt3 * jnp.exp(bend - cumulative), jnp.exp(cumulative),
+        up_dt, up_sl, after[0], after[1], dt3 * fall * later, jnp.exp(cumulative),
     ]
     rows = rows + [jnp.zeros_like(within)] * (ROWS - len(rows))
     table = jnp.stack(rows, axis=1).reshape(pairs, 2 * ROWS, tok)
@@ -369,47 +463,47 @@
         in_specs=vmem(3),
         out_specs=vmem(2),
         out_shape=[states, states],
-        scratch_shapes=[buffers] * 4 + [sems] * 4,
+        scratch_shapes=[
+            buffers, pltpu.VMEM((pairs, 8, 2 * dim), F32), buffers, buffers, buffers,
+            sems, sems, pltpu.SemaphoreType.DMA((2,)), sems, sems, sems, sems,
+        ],
         compiler_params=pltpu.CompilerParams(collective_id=1, has_side_effects=True),
         name="state_chain",
     )(block_state, block_grad, decay)
 
     skip_row = jnp.repeat(d_skip, dim).reshape(1, width)
-    dx, dbc, weighted, small = pl.pallas_call(
+    share = depth // pairs
+    dx, dbc, weighted, small, turned = pl.pallas_call(
         partial(group_kernel, groups),
         grid=(pairs,),
         in_specs=[
             wide, wide, whole, whole, tab_spec,
             pl.BlockSpec((1, 2 * dim), lambda i: (0, i)), square, square,
+            pl.BlockSpec((tok, share), lambda i: (0, i)),
         ],
         out_specs=[
             wide,
-            pl.BlockSpec((tok, 2 * state), lambda i: (0, 0)),
+            pl.BlockSpec((2 * state, tok), lambda i: (0, 0)),
             pl.BlockSpec((1, groups, 2 * ROWS, 6 * dim), lambda i: (i, 0, 0, 0)),
             pl.BlockSpec((1, groups, 8, GROUP), lambda i: (i, 0, 0, 0)),
+            pl.BlockSpec((share, tok), lambda i: (i, 0)),
         ],
         out_shape=[
             jax.ShapeDtypeStruct((tok, width), BF16),
-            jax.ShapeDtypeStruct((tok, 2 * state), F32),
+            jax.ShapeDtypeStruct((2 * state, tok), F32),
             jax.ShapeDtypeStruct((pairs, groups, 2 * ROWS, 6 * dim), F32),
             jax.ShapeDtypeStruct((pairs, groups, 8, GROUP), F32),
+            jax.ShapeDtypeStruct((depth, tok), BF16),
         ],
         scratch_shapes=[
             pltpu.VMEM((tok, GROUP), F32),
             pltpu.VMEM((tok, GROUP), F32),
             pltpu.VMEM((groups, state, 2 * dim), F32),
             pltpu.VMEM((groups, state, 2 * dim), F32),
+            pltpu.VMEM((tok, 2 * state), F32),
         ],
         name="group_terms",
-    )(ssm_input, grad_out, b_matrix, c_matrix, table, skip_row, state_in, grad_in)
-
-    owned = lax.psum_scatter(dbc, "mp", scatter_dimension=1, tiled=True).astype(BF16)
-    grad_wbc = lax.psum_scatter(
-        lax.dot_general(
-            layer_in, owned, (((0,), (0,)), ((), ())), preferred_element_type=F32
-        ),
-        "seq", scatter_dimension=0, tiled=True,
-    )
+    )(ssm_input, grad_out, b_matrix, c_matrix, table, skip_row, state_in, grad_in, layer_in)
 
     folded = jnp.sum(
         weighted.reshape(pairs, groups, 2, ROWS, 3, 2, dim), axis=(1, 6)
@@ -441,28 +535,36 @@
     block = depth // n
     half = block // 2
     q = 2
-    lt = layer_in.T.reshape(2 * n, half, tok)
+    m = lax.axis_size("mp")
+    cols = 2 * state // m
+    lt = turned.reshape(2 * n, half, tok)
+    around = pltpu.SemaphoreType.DMA((n, 2))
+    beside = pltpu.SemaphoreType.DMA((m,))
     ring = pltpu.SemaphoreType.DMA((n, 2, q))
     each = pltpu.SemaphoreType.DMA((n,))
-    grad_wx, totals = pl.pallas_call(
-        partial(ring_kernel, n, q),
-        in_specs=vmem(3),
-        out_specs=vmem(2),
+    grad_wx, grad_wbc, totals = pl.pallas_call(
+        partial(ring_kernel, n, m, q),
+        in_specs=vmem(4),
+        out_specs=vmem(3),
         out_shape=[
             jax.ShapeDtypeStruct((block, width), F32),
+            jax.ShapeDtypeStruct((block, cols), F32),
             jax.ShapeDtypeStruct((8, 128), F32),
         ],
         scratch_shapes=[
             pltpu.VMEM((n, 2, q, half, width // q), F32),
+            pltpu.VMEM((n, 2, half // 2, 2 * cols), F32),
+            pltpu.VMEM((cols, tok), BF16),
+            pltpu.VMEM((m, cols, tok), F32),
             pltpu.VMEM((n, 8, 128), F32),
-            ring, ring, each, each,
+            ring, ring, around, around, beside, beside, each, each,
         ],
         compiler_params=pltpu.CompilerParams(collective_id=2, has_side_effects=True),
         cost_estimate=pl.CostEstimate(
             flops=60 * 2 * tok * depth * width, bytes_accessed=2 * depth * width, transcendentals=0
         ),
         name="ring_projection",
-    )(lt, dx, stat)
+    )(lt, dx, dbc.reshape(m, cols, tok), stat)
     return (
         grad_wx, grad_wbc, rate * totals[0, :heads], totals[1, :heads], totals[2, :heads],
     )

time: 317 us -> 263 us (0.83)
  Pallas kernels: 259 us -> 238 us
  between operations: 14.4 us -> 0.97 us
  waiting for transfers between devices: 9.62 us -> 0 us
  local copies, waits for them, and re-layouts: 23.5 us -> 14.1 us
    pallas_call x1, Pallas kernels: 57.1 us -> 42.6 us  [on_device(): pl.pallas_call(partial(chain_kernel, n), in_specs=vmem(3), out_specs=vmem...]
    unnamed x4 -> x0, waiting for transfers between devices: 9.62 us -> none
    pallas_call x1, Pallas kernels: 150 us -> 141 us  [on_device(): pl.pallas_call(partial(ring_kernel, n, m, q), in_specs=vmem(4), out_specs...]
    transpose x1 -> x0, local copies, waits for them, and re-layouts: 6.32 us -> none  [on_device(): lt = layer_in.T.reshape(2 * n, half, tok)]
    unnamed x29 -> x22, local copies, waits for them, and re-layouts: 10.3 us -> 5.32 us
  transfers between devices with their start and end apart: 2 -> 0, of which waited for: 1 -> 0; matrix products, arithmetic and copies ran while one was open for 4% -> 0% of each run, Pallas kernels for 47% -> 0%
where the time goes in v2:
time: 263 us; the launch traced here: 262 us
  Pallas kernels  238 us (90%)
  local copies, waits for them, and re-layouts  14.1 us (5%)
  other arithmetic  8.77 us (3%)
    pallas_call x1, Pallas kernels, on_device(): pl.pallas_call(partial(ring_kernel, n, m, q), in_specs=vmem(4), out_specs...  141 us
    pallas_call x1, Pallas kernels, on_device(): pl.pallas_call(partial(group_kernel, groups), grid=(pairs,), in_specs=[wi...  42.7 us
    pallas_call x1, Pallas kernels, on_device(): pl.pallas_call(partial(chain_kernel, n), in_specs=vmem(3), out_specs=vmem...  42.6 us
    pallas_call x1, Pallas kernels, on_device(): pl.pallas_call(states_kernel, grid=(pairs,), in_specs=[wide, wide, whole,...  11.8 us
    unnamed x22, local copies, waits for them, and re-layouts  5.32 us

profile of v2, /device:TPU:0, one launch (start us, length us, event | category | flops | bytes accessed | tf_op | source)
XLA Modules:
  0.0 262.2 jit_solution(15640868273302494106)
XLA Ops:
  0.6 0.7 exponential_negate_fusion
  1.3 1.0 broadcast_multiply_fusion
  2.5 0.4 fusion
  3.0 0.2 slice_reduce_fusion.2
  3.2 0.2 exponential_reduce_fusion
  3.9 0.1 copy.119
  4.5 1.6 reshape.195.tab_ref
  6.1 11.8 %block_states.1 = (f32[10,128,128]{2,1,0:T(8,128)}, f32[10,128,128]{2,1,0:T(8,128)}) custom-call(bf16[768,1280]{1,0:T(8,128)(2,1)} %x_ref.3, bf16[768,1280]{1,0:T(8,128)(2,1)} %dy_ref.3, bf16[768,128]{1,0:T(8,128)(2,1)} %b_ref.3, bf16[768,128]{1,0:T(8,128)(2,1)} %c_ref.3, f32[10,32,768]{2,1,0:T(8,128)} %reshape.195.tab_ref), custom_call_target="tpu_custom_call" | custom-call | tf_op jit(solution)/shard_map/block_states/pallas_call | solution.py:448
  18.2 0.6 broadcast_in_dim.29.e_ref
  18.9 42.6 %state_chain.1 = (f32[10,128,128]{2,1,0:T(8,128)}, f32[10,128,128]{2,1,0:T(8,128)}) custom-call(f32[10,128,128]{2,1,0:T(8,128)} %get-tuple-element.29.s_ref, f32[10,128,128]{2,1,0:T(8,128)} %get-tuple-element.30.g_ref, f32[10,8,128]{2,1,0:T(8,128)} %broadcast_in_dim.29.e_ref), custom_call_target="tpu_custom_call" | custom-call | tf_op jit(solution)/shard_map/state_chain/pallas_call | solution.py:461
  61.6 0.7 reshape_reshape.4.skip_ref
  62.2 42.7 %group_terms.1 = (bf16[768,1280]{1,0:T(8,128)(2,1)}, f32[256,768]{1,0:T(8,128)}, f32[10,3,32,384]{3,2,1,0:T(8,128)}, f32[10,3,8,256]{3,2,1,0:T(8,128)}, bf16[2560,768]{1,0:T(8,128)(2,1)}) custom-call(bf16[768,1280]{1,0:T(8,128)(2,1)} %x_ref.3, bf16[768,1280]{1,0:T(8,128)(2,1)} %dy_ref.3, bf16[768,128]{1,0:T(8,128)(2,1)} %b_ref.3, bf16[768,128]{1,0:T(8,128)(2,1)} %c_ref.3, ...), custom_call_target="tpu_custom_call" | custom-call | tf_op jit(solution)/shard_map/group_terms/pallas_call | solution.py:476
  105.0 1.1 slice_bitcast_fusion.7
  106.1 0.2 slice_reduce_fusion.8
  106.3 1.1 slice_reduce_fusion.5
  107.5 0.1 reduce_sum.106
  107.7 0.2 slice_reduce_fusion.1
  107.9 1.5 reduce_sum.100
  109.4 0.6 reduce_sum.101
  110.1 1.4 reduce_sum.102
  111.4 0.2 fusion.31
  111.7 0.2 copy.143
  111.9 0.3 copy.144
  112.3 0.2 fusion.25
  112.5 1.0 slice_bitcast_fusion.4
  113.6 0.1 fusion.12
  114.0 0.6 select_maximum_fusion.st_ref
  114.6 140.7 %ring_projection.1 = (f32[320,1280]{1,0:T(8,128)}, f32[320,64]{1,0:T(8,128)}, f32[8,128]{1,0:T(8,128)}) custom-call(bf16[16,160,768]{2,1,0:T(8,128)(2,1)} %bitcast.103, bf16[768,1280]{1,0:T(8,128)(2,1)} %get-tuple-element.34.dx_ref, f32[4,64,768]{2,1,0:T(8,128)} %bitcast.104, f32[8,128]{1,0:T(8,128)} %select_maximum_fusion.st_ref), custom_call_target="tpu_custom_call" | custom-call | flops 301989888000 | bytes 6553600 | tf_op jit(solution)/shard_map/ring_projection/pallas_call | solution.py:545
  255.3 1.7 copy.138
  257.0 1.3 slice_bitcast_fusion.8
  258.3 1.2 bitcast_multiply_fusion.3
  259.5 2.7 %copy.170 = f32[320,1280]{1,0:T(8,128)} copy(f32[320,1280]{1,0:T(8,128)} %get-tuple-element.111) | data formatting | bytes 3276800
  (55 shorter events, 2.1 us)
Async XLA Ops:
  18.0 43.5 %copy-start = (f32[20]{0:T(128)S(1)}, f32[20]{0:T(128)}, u32[]{:S(2)}) copy-start(f32[20]{0:T(128)} %param.18) | copy-start | bytes 244
  111.4 2.3 copy-start.1
  114.6 143.7 %copy-start.2 = (f32[20]{0:T(128)S(1)}, f32[20]{0:T(128)}, u32[]{:S(2)}) copy-start(f32[20]{0:T(128)} %param.17) | copy-start | bytes 244

commit v3 on v2

--- a/solution.py
+++ b/solution.py
@@ -144,9 +144,15 @@
         total = jnp.where(first, intra[0], intra[1]) + g_end
         dx_ref[at, :] = (dt * total + skip_ref[...] * yf).astype(BF16)
         products = jnp.concatenate([backward, xd * g_end, xf * total], axis=1)
-        sums_ref[0, g] = nn(tab, products, HIGH)
+        here_sums = nn(tab, products, HIGH)
+        all_sums = here_sums if g == 0 else all_sums + here_sums
         small_ref[0, g, 4:5, :128] = jnp.sum(start * end, axis=0, keepdims=True)
         small_ref[0, g, 5:6, :128] = jnp.sum(xf * yf, axis=0, keepdims=True)
+
+    lane = lax.broadcasted_iota(jnp.int32, (products.shape[1], 128), 0)
+    slot = lax.broadcasted_iota(jnp.int32, (products.shape[1], 128), 1)
+    fold = jnp.where(lax.div(lane, 64) == slot, 1.0, 0.0)
+    sums_ref[0] = nn(all_sums, fold, HIGH)
 
     @pl.when(pair == pl.num_programs(0) - 1)
     def _():
@@ -484,14 +490,14 @@
         out_specs=[
             wide,
             pl.BlockSpec((2 * state, tok), lambda i: (0, 0)),
-            pl.BlockSpec((1, groups, 2 * ROWS, 6 * dim), lambda i: (i, 0, 0, 0)),
+            pl.BlockSpec((1, 2 * ROWS, 128), lambda i: (i, 0, 0)),
             pl.BlockSpec((1, groups, 8, GROUP), lambda i: (i, 0, 0, 0)),
             pl.BlockSpec((share, tok), lambda i: (i, 0)),
         ],
         out_shape=[
             jax.ShapeDtypeStruct((tok, width), BF16),
             jax.ShapeDtypeStruct((2 * state, tok), F32),
-            jax.ShapeDtypeStruct((pairs, groups, 2 * ROWS, 6 * dim), F32),
+            jax.ShapeDtypeStruct((pairs, 2 * ROWS, 128), F32),
             jax.ShapeDtypeStruct((pairs, groups, 8, GROUP), F32),
             jax.ShapeDtypeStruct((depth, tok), BF16),
         ],
@@ -505,9 +511,7 @@
         name="group_terms",
     )(ssm_input, grad_out, b_matrix, c_matrix, table, skip_row, state_in, grad_in, layer_in)
 
-    folded = jnp.sum(
-        weighted.reshape(pairs, groups, 2, ROWS, 3, 2, dim), axis=(1, 6)
-    )
+    folded = weighted[:, :, :6].reshape(pairs, 2, ROWS, 3, 2)
     own = jnp.stack([folded[:, 0, :, :, 0], folded[:, 1, :, :, 1]], axis=1)
     own = own.reshape(heads, ROWS, 3)
     row_w = jnp.stack(
@@ -534,7 +538,7 @@
 
     block = depth // n
     half = block // 2
-    q = 2
+    q = 5
     m = lax.axis_size("mp")
     cols = 2 * state // m
     lt = turned.reshape(2 * n, half, tok)

time: 263 us -> 257 us (0.977)
  other arithmetic: 8.77 us -> 5.84 us
    pallas_call x1, Pallas kernels: 42.7 us -> 39.7 us  [on_device(): pl.pallas_call(partial(group_kernel, groups), grid=(pairs,), in_specs=[wi...]
    reduce_sum x2 -> x0, other arithmetic: 2.91 us -> none  [on_device(): jnp.sum(weighted.reshape(pairs, groups, 2, ROWS, 3, 2, dim), axis=(1, 6))]
    unnamed x22 -> x20, local copies, waits for them, and re-layouts: 5.32 us -> 4.83 us
where the time goes in v3:
time: 257 us
  Pallas kernels  236 us (92%)
  local copies, waits for them, and re-layouts  13.9 us (5%)
  other arithmetic  5.84 us (2%)
    pallas_call x1, Pallas kernels, on_device(): pl.pallas_call(partial(ring_kernel, n, m, q), in_specs=vmem(4), out_specs...  142 us
    pallas_call x1, Pallas kernels, on_device(): pl.pallas_call(partial(chain_kernel, n), in_specs=vmem(3), out_specs=vmem...  42.6 us
    pallas_call x1, Pallas kernels, on_device(): pl.pallas_call(partial(group_kernel, groups), grid=(pairs,), in_specs=[wi...  39.7 us
    pallas_call x1, Pallas kernels, on_device(): pl.pallas_call(states_kernel, grid=(pairs,), in_specs=[wide, wide, whole,...  11.8 us

profile of v3, /device:TPU:0, one launch (start us, length us, event | category | flops | bytes accessed | tf_op | source)
XLA Modules:
  0.0 256.8 jit_solution(2871879695639187958)
XLA Ops:
  0.6 0.7 exponential_negate_fusion
  1.3 1.0 broadcast_multiply_fusion
  2.5 0.4 fusion
  3.0 0.2 slice_reduce_fusion.2
  3.2 0.2 exponential_reduce_fusion
  3.4 0.1 fusion.22
  3.9 0.1 copy.101
  4.1 0.1 slice_subtract_fusion
  4.4 0.1 broadcast_dynamic-update-slice_fusion
  4.5 1.6 reshape.196.tab_ref
  6.1 11.8 %block_states.1 = (f32[10,128,128]{2,1,0:T(8,128)}, f32[10,128,128]{2,1,0:T(8,128)}) custom-call(bf16[768,1280]{1,0:T(8,128)(2,1)} %x_ref.3, bf16[768,1280]{1,0:T(8,128)(2,1)} %dy_ref.3, bf16[768,128]{1,0:T(8,128)(2,1)} %b_ref.3, bf16[768,128]{1,0:T(8,128)(2,1)} %c_ref.3, f32[10,32,768]{2,1,0:T(8,128)} %reshape.196.tab_ref), custom_call_target="tpu_custom_call" | custom-call | tf_op jit(solution)/shard_map/block_states/pallas_call | solution.py:454
  18.2 0.6 broadcast_in_dim.29.e_ref
  18.8 42.6 %state_chain.1 = (f32[10,128,128]{2,1,0:T(8,128)}, f32[10,128,128]{2,1,0:T(8,128)}) custom-call(f32[10,128,128]{2,1,0:T(8,128)} %get-tuple-element.29.s_ref, f32[10,128,128]{2,1,0:T(8,128)} %get-tuple-element.30.g_ref, f32[10,8,128]{2,1,0:T(8,128)} %broadcast_in_dim.29.e_ref), custom_call_target="tpu_custom_call" | custom-call | tf_op jit(solution)/shard_map/state_chain/pallas_call | solution.py:467
  61.5 0.7 reshape_reshape.4.skip_ref
  62.2 39.7 %group_terms.1 = (bf16[768,1280]{1,0:T(8,128)(2,1)}, f32[256,768]{1,0:T(8,128)}, f32[10,32,128]{2,1,0:T(8,128)}, f32[10,3,8,256]{3,2,1,0:T(8,128)}, bf16[2560,768]{1,0:T(8,128)(2,1)}) custom-call(bf16[768,1280]{1,0:T(8,128)(2,1)} %x_ref.3, bf16[768,1280]{1,0:T(8,128)(2,1)} %dy_ref.3, bf16[768,128]{1,0:T(8,128)(2,1)} %b_ref.3, bf16[768,128]{1,0:T(8,128)(2,1)} %c_ref.3, ...), custom_call_target="tpu_custom_call" | custom-call | tf_op jit(solution)/shard_map/group_terms/pallas_call | solution.py:482
  101.9 1.0 slice_bitcast_fusion.4
  102.9 0.1 fusion.12
  103.0 1.1 slice_bitcast_fusion.9
  104.2 0.2 slice_reduce_fusion.8
  104.4 1.1 slice_reduce_fusion.5
  105.4 0.1 reshape_squeeze.4
  105.5 0.1 reduce_sum.87
  105.7 0.2 slice_reduce_fusion.1
  105.9 1.0 copy.115
  107.0 0.1 reshape.199
  107.2 0.2 fusion.25
  107.7 0.6 select_maximum_fusion.st_ref
  108.4 141.5 %ring_projection.1 = (f32[320,1280]{1,0:T(8,128)}, f32[320,64]{1,0:T(8,128)}, f32[8,128]{1,0:T(8,128)}) custom-call(bf16[16,160,768]{2,1,0:T(8,128)(2,1)} %bitcast.107, bf16[768,1280]{1,0:T(8,128)(2,1)} %get-tuple-element.34.dx_ref, f32[4,64,768]{2,1,0:T(8,128)} %bitcast.108, f32[8,128]{1,0:T(8,128)} %select_maximum_fusion.st_ref), custom_call_target="tpu_custom_call" | custom-call | flops 301989888000 | bytes 6553600 | tf_op jit(solution)/shard_map/ring_projection/pallas_call | solution.py:549
  249.9 1.7 copy.120
  251.6 1.3 slice_bitcast_fusion.10
  252.9 1.2 bitcast_multiply_fusion.3
  254.1 2.7 %copy.149 = f32[320,1280]{1,0:T(8,128)} copy(f32[320,1280]{1,0:T(8,128)} %get-tuple-element.106) | data formatting | bytes 3276800
  (52 shorter events, 1.7 us)
Async XLA Ops:
  18.0 43.5 %copy-start = (f32[20]{0:T(128)S(1)}, f32[20]{0:T(128)}, u32[]{:S(2)}) copy-start(f32[20]{0:T(128)} %param.18) | copy-start | bytes 244
  101.8 5.6 %copy-start.1 = (f32[20]{0:T(128)S(1)}, f32[20]{0:T(128)}, u32[]{:S(2)}) copy-start(f32[20]{0:T(128)} %param.17) | copy-start | bytes 244
  108.4 144.5 %copy-start.2 = (f32[20]{0:T(128)S(1)}, f32[20]{0:T(128)}, u32[]{:S(2)}) copy-start(f32[20]{0:T(128)} %param.17) | copy-start | bytes 244
